TPU v7x, 128 devices: a whole 4x4x4 slice. The times are simulated.
128 devices in a mesh: expert: 16 (over x_hi, y, core), row: 8 (over z, x_lo).
Axes of the slice: x: 4 (x_hi: 2, x_lo: 2; x = x_hi * 2 + x_lo), y: 4, z: 4, core: 2. Of those that a mesh axis runs over, the one named last changes fastest.
Arguments:
- weights: bfloat16 [16, 7168, 2048], P('expert', 'row'), may hold values from -6 to 6
- left_bits: int32 [16, 7168], P('expert', 'row'), may hold values from 0 to 1
- right_bits: int32 [16, 2048], P('expert'), may hold values from 0 to 1
- groups: int32 [16, 2048], P('expert'), may hold values from 0 to 15, never falling along the last dimension, each value on 1 to 256 neighbouring positions
Outputs:
- scaled: bfloat16 [16, 7168, 2048], P('expert', 'row')
- block_error: float32 [16, 7168, 256], P('expert', 'row')
- scales: float32 [16, 16], P('expert')
- expert_error: float32 [16], P('expert')
- total_error: float32 [], replicated
Inputs may be any that keep to these rules, and one draw needn't show every extreme that they name: Along each expert's 2048 columns the group number never falls; each of the 16 groups holds 1 to 256 columns.
All inputs are finite; a program needn't handle non-finite values.
Results may differ from a plain program's by a relative error of at most 0.0091.
Values may be sent and summed in bfloat16 or wider, within the bound.
A program may use at most 128 MiB of HBM per device.

v0:
```python
import math
import jax
import jax.numpy as jnp
from jax import lax
from jax.sharding import PartitionSpec as P

D = 7168
FF = 2048
HB = 128
OUTER = 16
GROUPS = 16
BLOCKS = 56


def from_everyone(value, axis):
    peers = lax.axis_size(axis)
    return lax.all_to_all(
        jnp.broadcast_to(value[None], (peers, *value.shape)), axis, 0, 0, tiled=True
    )


def over_copies(value, axis):
    everything = from_everyone(value, axis)
    return jnp.max(everything, axis=0)


def taken_together(value, axis):
    return from_everyone(value, axis).sum(axis=0)


def sylvester(order):
    row_index = jnp.arange(order, dtype=jnp.int32)[:, None]
    col_index = jnp.arange(order, dtype=jnp.int32)[None, :]
    common = jnp.bitwise_and(row_index, col_index)
    parity = jnp.zeros((order, order), jnp.int32)
    for bit_pos in range(order.bit_length() - 1):
        parity = parity + jnp.bitwise_and(jnp.right_shift(common, bit_pos), 1)
    return (1 - 2 * jnp.bitwise_and(parity, 1)).astype(jnp.float32)


def cosine_block(order):
    first = jnp.arange(order, dtype=jnp.float32)[:, None]
    second = jnp.arange(order, dtype=jnp.float32)[None, :]
    table = math.sqrt(2.0 / order) * jnp.cos(math.pi * (2.0 * second + 1.0) * first / (2.0 * order))
    return jnp.where(first == 0.0, table * math.sqrt(0.5), table)


def coset_error(values):
    nearest = jnp.floor(values + 0.5)
    offset = values - nearest
    squares = jnp.sum(offset * offset, axis=-1)
    largest = jnp.max(jnp.abs(offset), axis=-1)
    parity = jnp.mod(jnp.sum(nearest, axis=-1), 2.0)
    return jnp.where(parity > 0.5, squares + 1.0 - 2.0 * largest, squares)


def lattice_error(values):
    octets = values.reshape(values.shape[:-1] + (values.shape[-1] // 8, 8))
    return jnp.minimum(coset_error(octets), coset_error(octets - 0.5))


def row_transform(mixed_rows, row_hadamard):
    turned = jnp.einsum("eibf,bk->eikf", mixed_rows, row_hadamard, precision=lax.Precision.HIGHEST)
    return turned / math.sqrt(HB)


def weight_of_rows(first_row, count):
    positions = (first_row + jnp.arange(count, dtype=jnp.int32)).astype(jnp.float32)
    return (1.0 + 4.0 * (positions + 0.5) / D) / 3.0


def group_scale(rotated, group_cols):
    column_peak = jnp.max(jnp.abs(rotated), axis=1)
    group_ids = jnp.arange(GROUPS, dtype=jnp.int32)
    in_group = group_cols[:, None, :] == group_ids[None, :, None]
    partial_peak = jnp.max(jnp.where(in_group, column_peak[:, None, :], 0.0), axis=2)
    group_peak = jnp.maximum(over_copies(partial_peak, "row"), 1.0)
    column_scale = jnp.sum(jnp.where(in_group, (2.0 / group_peak)[:, :, None], 0.0), axis=1)
    return (group_peak, column_scale)


def body(weights, left_bits, right_bits, groups):
    experts, local_rows, width = weights.shape
    blocks_here = local_rows // HB
    column_hadamard = sylvester(width // OUTER).astype(jnp.bfloat16)
    outer_hadamard = sylvester(OUTER)
    row_hadamard = sylvester(HB)
    block_matrix = cosine_block(BLOCKS).astype(jnp.bfloat16)
    left_sign = (2 * left_bits - 1).astype(jnp.float32)
    right_sign = (2 * right_bits - 1).astype(jnp.float32)
    signed = (weights.astype(jnp.float32) * left_sign[:, :, None] * right_sign[:, None, :]).astype(
        jnp.bfloat16
    )
    shaped = signed.reshape(experts, local_rows, OUTER, width // OUTER)
    inner = jnp.einsum("erpq,qs->erps", shaped, column_hadamard, preferred_element_type=jnp.float32)
    outer = jnp.einsum("erps,pt->erts", inner, outer_hadamard, precision=lax.Precision.HIGHEST)
    columns = (outer.reshape(experts, local_rows, width) / math.sqrt(FF)).astype(jnp.bfloat16)
    blocked = columns.reshape(experts, blocks_here, HB, width)
    column_slab = lax.all_to_all(blocked, "row", split_axis=3, concat_axis=1, tiled=True)
    mixed_rows = jnp.einsum(
        "ij,ejbf->eibf", block_matrix, column_slab, preferred_element_type=jnp.float32
    )
    turned = row_transform(mixed_rows, row_hadamard)
    rotated = lax.all_to_all(
        turned.astype(jnp.bfloat16), "row", split_axis=1, concat_axis=3, tiled=True
    ).astype(turned.dtype)
    rotated = rotated.reshape(experts, local_rows, width)
    group_peak, column_scale = group_scale(rotated, groups)
    values = rotated * column_scale[:, None, :]
    block_errors = lattice_error(values)
    row_weight = weight_of_rows(lax.axis_index("row") * local_rows, local_rows)
    partial_error = jnp.sum(block_errors * row_weight[None, :, None], axis=(1, 2)) / (D * FF // 8)
    scaled = values.astype(jnp.bfloat16)
    expert_count = experts * lax.axis_size("expert")
    expert_error = taken_together(partial_error, "row")
    total_error = taken_together(jnp.sum(expert_error), "expert") / expert_count
    return (scaled, block_errors, group_peak / 2.0, expert_error, total_error)


def solution(mesh):
    placed = (P("expert", "row", None), P("expert", "row"), P("expert", None), P("expert", None))
    return jax.shard_map(
        body,
        mesh=mesh,
        in_specs=placed,
        out_specs=(
            P("expert", "row", None),
            P("expert", "row", None),
            P("expert", None),
            P("expert"),
            P(),
        ),
        check_vma=False,
    )
```

profile of v0, /device:TPU:1, one launch (start us, length us, event | category | flops | bytes accessed | tf_op | source)
XLA Modules:
  0.0 254.1 jit_solution(4140201884117918043)
XLA Ops:
  2.0 3.1 %fusion.4 = bf16[112,8,16,128]{3,1,2,0:T(8,128)(2,1)S(1)} fusion(bf16[1,896,2048]{2,1,0:T(8,128)(2,1)} %param.4, f32[2048]{0:T(1024)S(1)} %bitcast.116, f32[896]{0:T(1024)S(1)} %convert_reduce_fusion), kind=kLoop, calls=%fused_computation.16 | loop fusion | flops 7340032 | bytes 7351808
  7.5 8.3 %fusion.5 = bf16[1,896,16,128]{3,2,1,0:T(8,128)(2,1)} fusion(f32[896,16,128]{2,1,0:T(8,128)S(1)} %fusion.24), kind=kOutput, calls=%fused_computation.17 | convolution fusion | flops 355995648 | bytes 11010048 | tf_op jit(solution)/shard_map/erps,pt->erts/dot_general | solution.py:96
  15.8 6.7 %convert_element_type.172 = bf16[1,7,128,2048]{3,2,1,0:T(8,128)(2,1)} reshape(bf16[1,896,16,128]{3,2,1,0:T(8,128)(2,1)} %fusion.5) | data formatting | bytes 7340032 | tf_op jit(solution)/shard_map/convert_element_type | solution.py:97
  22.5 6.5 %copy.44 = bf16[1,7,128,2048]{2,1,0,3:T(8,128)(2,1)} copy(bf16[1,7,128,2048]{3,2,1,0:T(8,128)(2,1)} %convert_element_type.172) | data formatting | bytes 7340032 | tf_op jit(solution)/shard_map/convert_element_type | solution.py:97
  29.0 6.8 %all-to-all-start = ((bf16[1,7,128,2048]{2,1,0,3:T(8,128)(2,1)}), bf16[1,7,128,2048]{2,1,0,3:T(8,128)(2,1)}, u32[]{:S(2)}, u32[]{:S(2)}) async-start(bf16[1,7,128,2048]{2,1,0,3:T(8,128)(2,1)} %copy.44), calls=%async_computation | async-start | bytes 8388608 | tf_op jit(solution)/shard_map/all_to_all | solution.py:99
  35.8 48.7 %all-to-all-done = bf16[1,7,128,2048]{2,1,0,3:T(8,128)(2,1)} async-done(((bf16[1,7,128,2048]{2,1,0,3:T(8,128)(2,1)}), bf16[1,7,128,2048]{2,1,0,3:T(8,128)(2,1)}, u32[]{:S(2)}, u32[]{:S(2)}) %all-to-all-start) | async-done | bytes 3670048 | tf_op jit(solution)/shard_map/all_to_all | solution.py:99
  84.5 4.5 %copy.45 = bf16[1,7,128,2048]{2,3,1,0:T(8,128)(2,1)} copy(bf16[1,7,128,2048]{2,1,0,3:T(8,128)(2,1)} %all-to-all-done) | data formatting | bytes 7340032 | tf_op jit(solution)/shard_map/all_to_all | solution.py:99
  89.0 6.3 %copy.46 = bf16[1,8,7,128,256]{4,3,2,1,0:T(8,128)(2,1)} copy(bf16[1,8,7,128,256]{3,4,1,2,0:T(8,128)(2,1)} %bitcast.110) | data formatting | bytes 7340032 | tf_op jit(solution)/shard_map/all_to_all | solution.py:99
  95.3 5.1 %fusion.9 = f32[56,128,256]{2,0,1:T(8,128)S(1)} fusion(bf16[56,128,256]{2,1,0:T(8,128)(2,1)} %bitcast.109, f32[56]{0:T(128)S(1)} %add_multiply_fusion.1, pred[56]{0:T(512)(128)(4,1)S(1)} %iota_compare_fusion.1), kind=kOutput, calls=%fused_computation.21 | convolution fusion | flops 205539712 | bytes 11010328 | tf_op jit(solution)/shard_map/ij,ejbf->eibf/dot_general | solution.py:100
  100.4 9.8 %fusion.6 = bf16[1,56,128,256]{3,2,0,1:T(8,128)(2,1)} fusion(f32[56,128,256]{2,0,1:T(8,128)S(1)} %fusion.9), kind=kOutput, calls=%fused_computation.18 | convolution fusion | flops 2822651904 | bytes 11010048 | tf_op jit(solution)/shard_map/eibf,bk->eikf/dot_general | solution.py:63
  110.2 4.7 %all-to-all-start.1 = ((bf16[1,56,128,256]{3,2,0,1:T(8,128)(2,1)}), bf16[1,56,128,256]{3,2,0,1:T(8,128)(2,1)}, u32[]{:S(2)}, u32[]{:S(2)}) async-start(bf16[1,56,128,256]{3,2,0,1:T(8,128)(2,1)} %fusion.6), calls=%async_computation.1 | async-start | bytes 7340032 | tf_op jit(solution)/shard_map/all_to_all | solution.py:104
  114.9 42.1 %all-to-all-done.1 = bf16[1,56,128,256]{3,2,0,1:T(8,128)(2,1)} async-done(((bf16[1,56,128,256]{3,2,0,1:T(8,128)(2,1)}), bf16[1,56,128,256]{3,2,0,1:T(8,128)(2,1)}, u32[]{:S(2)}, u32[]{:S(2)}) %all-to-all-start.1) | async-done | bytes 3670048 | tf_op jit(solution)/shard_map/all_to_all | solution.py:104
  157.0 3.2 %abs_reduce_fusion.2 = f32[56,256]{1,0:T(8,128)S(1)} fusion(bf16[1,56,128,256]{3,2,0,1:T(8,128)(2,1)} %all-to-all-done.1), kind=kLoop, calls=%fused_computation.11 | loop fusion | flops 5490688 | bytes 3727360 | tf_op jit(solution)/shard_map/reduce_max | solution.py:73
  161.0 4.6 %all-to-all-start.2 = ((f32[8,1,16]{2,1,0:T(1,128)}), f32[8,1,16]{2,1,0:T(1,128)S(1)}, u32[]{:S(2)}, u32[]{:S(2)}) async-start(f32[8,1,16]{2,1,0:T(1,128)} %broadcast_in_dim.42), calls=%async_computation.2 | async-start | bytes 8192 | tf_op jit(solution)/shard_map/all_to_all | solution.py:17
  165.5 7.0 %copy.50 = f32[1,8,7,128,256]{3,2,4,1,0:T(8,128)} copy(bf16[1,8,7,128,256]{4,3,2,1,0:T(8,128)(2,1)} %bitcast.95) | data formatting | bytes 11010048 | tf_op jit(solution)/shard_map/convert_element_type | solution.py:106
  172.6 9.2 %reshape.657 = f32[1,896,256,8]{1,3,2,0:T(8,128)} reshape(f32[1,7,128,8,256]{2,1,4,3,0:T(8,128)} %bitcast.107) | data formatting | bytes 14680064 | tf_op jit(solution)/shard_map/convert_element_type | solution.py:106
  181.8 9.3 %reshape.664 = f32[1,896,2048]{1,2,0:T(8,128)} reshape(f32[1,7,128,8,256]{2,1,4,3,0:T(8,128)} %bitcast.108) | data formatting | bytes 14680064 | tf_op jit(solution)/shard_map/convert_element_type | solution.py:106
  191.1 8.6 %copy.58 = f32[1,896,2048]{2,1,0:T(8,128)} copy(f32[1,896,2048]{1,2,0:T(8,128)} %reshape.664) | data formatting | bytes 14680064 | tf_op jit(solution)/shard_map/convert_element_type | solution.py:106
  200.4 19.5 %fusion.3 = (f32[896,256]{0,1:T(8,128)S(1)}, f32[896,256]{0,1:T(8,128)S(1)}, f32[896,256]{0,1:T(8,128)S(1)}, f32[896,256]{0,1:T(8,128)S(1)}, f32[896,256]{0,1:T(8,128)S(1)}, /*index=5*/f32[896,256]{0,1:T(8,128)S(1)}) fusion(f32[1,896,256,8]{1,3,2,0:T(8,128)} %reshape.657, f32[256,8]{1,0:T(8,128)S(1)} %mul.272), kind=kLoop, calls=%fused_computation.9 | loop fusion | flops 29818880 | bytes 12853248 | tf_op jit(solution)/shard_map/reduce_sum | solution.py:53
  219.9 1.9 multiply_reduce_fusion.2
  223.1 5.1 %all-to-all-start.3 = ((f32[8,1,1]{2,1,0:T(1,128)}), f32[8,1,1]{2,1,0:T(1,128)S(1)}, u32[]{:S(2)}, u32[]{:S(2)}) async-start(f32[8,1,1]{2,1,0:T(1,128)} %broadcast_in_dim.44), calls=%async_computation.3 | async-start | bytes 8192 | tf_op jit(solution)/shard_map/all_to_all | solution.py:17
  228.2 5.9 %multiply_convert_fusion = bf16[1,896,2048]{2,1,0:T(8,128)(2,1)} fusion(f32[1,896,2048]{2,1,0:T(8,128)} %copy.58, f32[2048]{0:T(1024)S(1)} %select_reduce_fusion), kind=kLoop, calls=%fused_computation.10 | loop fusion | flops 3670016 | bytes 11018240 | tf_op jit(solution)/shard_map/convert_element_type | solution.py:113
  236.0 8.7 %all-to-all-start.4 = ((f32[16,1,1]{2,1,0:T(1,128)}), f32[16,1,1]{2,1,0:T(1,128)S(1)}, u32[]{:S(2)}, u32[]{:S(2)}) async-start(f32[16,1,1]{2,1,0:T(1,128)} %broadcast_in_dim.45), calls=%async_computation.4 | async-start | bytes 16384 | tf_op jit(solution)/shard_map/all_to_all | solution.py:17
  245.9 5.8 %all-to-all-done.4 = f32[16,1,1]{2,1,0:T(1,128)S(1)} async-done(((f32[16,1,1]{2,1,0:T(1,128)}), f32[16,1,1]{2,1,0:T(1,128)S(1)}, u32[]{:S(2)}, u32[]{:S(2)}) %all-to-all-start.4) | async-done | bytes 96 | tf_op jit(solution)/shard_map/all_to_all | solution.py:17
  (25 shorter events, 9.6 us)
Async XLA Ops:
  29.0 55.5 %all-to-all-start = ((bf16[1,7,128,2048]{2,1,0,3:T(8,128)(2,1)}), bf16[1,7,128,2048]{2,1,0,3:T(8,128)(2,1)}, u32[]{:S(2)}, u32[]{:S(2)}) async-start(bf16[1,7,128,2048]{2,1,0,3:T(8,128)(2,1)} %copy.44), calls=%async_computation | async-start | bytes 8388608 | tf_op jit(solution)/shard_map/all_to_all | solution.py:99
  110.2 50.1 %copy-start = (s32[1,2048]{1,0:T(1,128)S(1)}, s32[1,2048]{1,0:T(1,128)}, u32[]{:S(2)}) copy-start(s32[1,2048]{1,0:T(1,128)} %param.7) | copy-start | bytes 24580
  110.2 46.8 %all-to-all-start.1 = ((bf16[1,56,128,256]{3,2,0,1:T(8,128)(2,1)}), bf16[1,56,128,256]{3,2,0,1:T(8,128)(2,1)}, u32[]{:S(2)}, u32[]{:S(2)}) async-start(bf16[1,56,128,256]{3,2,0,1:T(8,128)(2,1)} %fusion.6), calls=%async_computation.1 | async-start | bytes 7340032 | tf_op jit(solution)/shard_map/all_to_all | solution.py:104
  161.0 38.7 %all-to-all-start.2 = ((f32[8,1,16]{2,1,0:T(1,128)}), f32[8,1,16]{2,1,0:T(1,128)S(1)}, u32[]{:S(2)}, u32[]{:S(2)}) async-start(f32[8,1,16]{2,1,0:T(1,128)} %broadcast_in_dim.42), calls=%async_computation.2 | async-start | bytes 8192 | tf_op jit(solution)/shard_map/all_to_all | solution.py:17
  223.1 11.1 %all-to-all-start.3 = ((f32[8,1,1]{2,1,0:T(1,128)}), f32[8,1,1]{2,1,0:T(1,128)S(1)}, u32[]{:S(2)}, u32[]{:S(2)}) async-start(f32[8,1,1]{2,1,0:T(1,128)} %broadcast_in_dim.44), calls=%async_computation.3 | async-start | bytes 8192 | tf_op jit(solution)/shard_map/all_to_all | solution.py:17
  236.0 15.7 %all-to-all-start.4 = ((f32[16,1,1]{2,1,0:T(1,128)}), f32[16,1,1]{2,1,0:T(1,128)S(1)}, u32[]{:S(2)}, u32[]{:S(2)}) async-start(f32[16,1,1]{2,1,0:T(1,128)} %broadcast_in_dim.45), calls=%async_computation.4 | async-start | bytes 16384 | tf_op jit(solution)/shard_map/all_to_all | solution.py:17
where the time goes:
time: 256 us; the launch traced here: 254 us
  waiting for transfers between devices  96.6 us (38%)
  local copies, waits for them, and re-layouts  63.1 us (25%)
  other arithmetic  37 us (14%)
  starting transfers between devices  29.9 us (12%)
  matrix products  24.4 us (10%)
  between operations  3.17 us (1%)
    all_to_all x1, waiting for transfers between devices, body(): lax.all_to_all(blocked, 'row', split_axis=3, concat_axis=1, tiled=True)  48.7 us
    all_to_all x1, waiting for transfers between devices, body(): lax.all_to_all(turned.astype(jnp.bfloat16), 'row', split_axis=1, concat_a...  42.1 us
    convert_element_type x4, local copies, waits for them, and re-layouts, body(): rotated = lax.all_to_all(turned.astype(jnp.bfloat16), 'row', split_axis=1...  34.1 us
    reduce_sum x1, other arithmetic, coset_error(): parity = jnp.mod(jnp.sum(nearest, axis=-1), 2.0)  19.5 us
    all_to_all x3, starting transfers between devices, from_everyone(): lax.all_to_all(jnp.broadcast_to(value[None], (peers, *value.shape)), axis...  18.4 us
    convert_element_type x2, local copies, waits for them, and re-layouts, body(): (outer.reshape(experts, local_rows, width) / math.sqrt(FF)).astype(jnp.bf...  13.1 us
    all_to_all x2, local copies, waits for them, and re-layouts, body(): lax.all_to_all(blocked, 'row', split_axis=3, concat_axis=1, tiled=True)  10.8 us
    dot_general x1, matrix products, row_transform(): jnp.einsum('eibf,bk->eikf', mixed_rows, row_hadamard, precision=lax.Preci...  9.8 us
  transfers between devices with their start and end apart: 5, of which 3 were waited for; matrix products, arithmetic and copies ran while one was open for 16% of the time, Pallas kernels for 0%

commit v1 on v0

--- a/solution.py
+++ b/solution.py
@@ -10,6 +10,12 @@
 OUTER = 16
 GROUPS = 16
 BLOCKS = 56
+
+
+def swap_blocks(x, mesh_axis, split, join):
+    shards = jnp.split(x, lax.axis_size(mesh_axis), axis=split)
+    received = lax.all_to_all(jnp.stack(shards), mesh_axis, 0, 0)
+    return jnp.concatenate(received, axis=join)
 
 
 def from_everyone(value, axis):
@@ -96,7 +102,7 @@
     outer = jnp.einsum("erps,pt->erts", inner, outer_hadamard, precision=lax.Precision.HIGHEST)
     columns = (outer.reshape(experts, local_rows, width) / math.sqrt(FF)).astype(jnp.bfloat16)
     blocked = columns.reshape(experts, blocks_here, HB, width)
-    column_slab = lax.all_to_all(blocked, "row", split_axis=3, concat_axis=1, tiled=True)
+    column_slab = swap_blocks(blocked, "row", 3, 1)
     mixed_rows = jnp.einsum(
         "ij,ejbf->eibf", block_matrix, column_slab, preferred_element_type=jnp.float32
     )

time: 256 us -> 247 us (0.965)
  waiting for transfers between devices: 96.6 us -> 91 us
  local copies, waits for them, and re-layouts: 63.1 us -> 60.3 us
    unnamed x5 -> x12, local copies, waits for them, and re-layouts: 2.44 us -> 15.1 us
    all_to_all x2 -> x0, local copies, waits for them, and re-layouts: 10.8 us -> none  [body(): lax.all_to_all(blocked, 'row', split_axis=3, concat_axis=1, tiled=True)]
    convert_element_type x2 -> x1, local copies, waits for them, and re-layouts: 13.1 us -> 6.67 us  [body(): (outer.reshape(experts, local_rows, width) / math.sqrt(FF)).astype(jnp.bf...]
    all_to_all x1, waiting for transfers between devices: 48.7 us -> 43.1 us  [swap_blocks(): received = lax.all_to_all(jnp.stack(shards), mesh_axis, 0, 0)]
  transfers between devices with their start and end apart: 5 -> 5, of which waited for: 3 -> 3; matrix products, arithmetic and copies ran while one was open for 16% -> 17% of each run, Pallas kernels for 0% -> 0%
where the time goes in v1:
time: 247 us; the launch traced here: 246 us
  waiting for transfers between devices  91 us (37%)
  local copies, waits for them, and re-layouts  60.3 us (24%)
  other arithmetic  37 us (15%)
  starting transfers between devices  29.8 us (12%)
  matrix products  24.4 us (10%)
  between operations  3.18 us (1%)
    all_to_all x1, waiting for transfers between devices, swap_blocks(): received = lax.all_to_all(jnp.stack(shards), mesh_axis, 0, 0)  43.1 us
    all_to_all x1, waiting for transfers between devices, body(): lax.all_to_all(turned.astype(jnp.bfloat16), 'row', split_axis=1, concat_a...  42.1 us
    convert_element_type x4, local copies, waits for them, and re-layouts, body(): rotated = lax.all_to_all(turned.astype(jnp.bfloat16), 'row', split_axis=1...  34.1 us
    reduce_sum x1, other arithmetic, coset_error(): parity = jnp.mod(jnp.sum(nearest, axis=-1), 2.0)  19.5 us
    all_to_all x3, starting transfers between devices, from_everyone(): lax.all_to_all(jnp.broadcast_to(value[None], (peers, *value.shape)), axis...  18.4 us
    unnamed x12, local copies, waits for them, and re-layouts  15.1 us
    dot_general x1, matrix products, row_transform(): jnp.einsum('eibf,bk->eikf', mixed_rows, row_hadamard, precision=lax.Preci...  9.8 us
    dot_general x1, matrix products, body(): jnp.einsum('erps,pt->erts', inner, outer_hadamard, precision=lax.Precisio...  8.35 us
  transfers between devices with their start and end apart: 5, of which 3 were waited for; matrix products, arithmetic and copies ran while one was open for 17% of the time, Pallas kernels for 0%

profile of v1, /device:TPU:1, one launch (start us, length us, event | category | flops | bytes accessed | tf_op | source)
XLA Modules:
  0.0 245.6 jit_solution(8982546404757824021)
XLA Ops:
  2.0 3.1 %fusion.4 = bf16[112,8,16,128]{3,1,2,0:T(8,128)(2,1)S(1)} fusion(bf16[1,896,2048]{2,1,0:T(8,128)(2,1)} %param.4, f32[2048]{0:T(1024)S(1)} %bitcast.143, f32[896]{0:T(1024)S(1)} %convert_reduce_fusion), kind=kLoop, calls=%fused_computation.16 | loop fusion | flops 7340032 | bytes 7351808
  7.5 8.3 %fusion.5 = bf16[1,896,16,128]{3,2,1,0:T(8,128)(2,1)} fusion(f32[896,16,128]{2,1,0:T(8,128)S(1)} %fusion.32), kind=kOutput, calls=%fused_computation.17 | convolution fusion | flops 355995648 | bytes 11010048 | tf_op jit(solution)/shard_map/erps,pt->erts/dot_general | solution.py:102
  15.8 6.7 %convert_element_type.172 = bf16[1,7,128,2048]{3,2,1,0:T(8,128)(2,1)} reshape(bf16[1,896,16,128]{3,2,1,0:T(8,128)(2,1)} %fusion.5) | data formatting | bytes 7340032 | tf_op jit(solution)/shard_map/convert_element_type | solution.py:103
  26.1 1.8 fusion.26
  27.9 1.8 fusion.25
  29.8 1.8 fusion.24
  37.0 6.8 %all-to-all-start = ((bf16[8,1,7,128,256]{4,3,2,1,0:T(8,128)(2,1)}), bf16[8,1,7,128,256]{4,3,2,1,0:T(8,128)(2,1)}, u32[]{:S(2)}, u32[]{:S(2)}) async-start(bf16[8,1,7,128,256]{4,3,2,1,0:T(8,128)(2,1)} %fusion.21), calls=%async_computation | async-start | bytes 7340032 | tf_op jit(solution)/shard_map/all_to_all | solution.py:17
  43.8 43.1 %all-to-all-done = bf16[8,1,7,128,256]{4,3,2,1,0:T(8,128)(2,1)} async-done(((bf16[8,1,7,128,256]{4,3,2,1,0:T(8,128)(2,1)}), bf16[8,1,7,128,256]{4,3,2,1,0:T(8,128)(2,1)}, u32[]{:S(2)}, u32[]{:S(2)}) %all-to-all-start) | async-done | bytes 3670048 | tf_op jit(solution)/shard_map/all_to_all | solution.py:17
  86.9 5.1 %fusion.9 = f32[56,128,256]{2,0,1:T(8,128)S(1)} fusion(bf16[56,128,256]{2,1,0:T(8,128)(2,1)} %bitcast.14, f32[56]{0:T(128)S(1)} %add_multiply_fusion.1, pred[56]{0:T(512)(128)(4,1)S(1)} %iota_compare_fusion.1), kind=kOutput, calls=%fused_computation.21 | convolution fusion | flops 205539712 | bytes 11010328 | tf_op jit(solution)/shard_map/ij,ejbf->eibf/dot_general | solution.py:106
  92.0 9.8 %fusion.6 = bf16[1,56,128,256]{3,2,0,1:T(8,128)(2,1)} fusion(f32[56,128,256]{2,0,1:T(8,128)S(1)} %fusion.9), kind=kOutput, calls=%fused_computation.18 | convolution fusion | flops 2822651904 | bytes 11010048 | tf_op jit(solution)/shard_map/eibf,bk->eikf/dot_general | solution.py:69
  101.8 4.6 %all-to-all-start.1 = ((bf16[1,56,128,256]{3,2,0,1:T(8,128)(2,1)}), bf16[1,56,128,256]{3,2,0,1:T(8,128)(2,1)}, u32[]{:S(2)}, u32[]{:S(2)}) async-start(bf16[1,56,128,256]{3,2,0,1:T(8,128)(2,1)} %fusion.6), calls=%async_computation.1 | async-start | bytes 7340032 | tf_op jit(solution)/shard_map/all_to_all | solution.py:110
  106.3 42.1 %all-to-all-done.1 = bf16[1,56,128,256]{3,2,0,1:T(8,128)(2,1)} async-done(((bf16[1,56,128,256]{3,2,0,1:T(8,128)(2,1)}), bf16[1,56,128,256]{3,2,0,1:T(8,128)(2,1)}, u32[]{:S(2)}, u32[]{:S(2)}) %all-to-all-start.1) | async-done | bytes 3670048 | tf_op jit(solution)/shard_map/all_to_all | solution.py:110
  148.5 3.2 %abs_reduce_fusion.2 = f32[56,256]{1,0:T(8,128)S(1)} fusion(bf16[1,56,128,256]{3,2,0,1:T(8,128)(2,1)} %all-to-all-done.1), kind=kLoop, calls=%fused_computation.11 | loop fusion | flops 5490688 | bytes 3727360 | tf_op jit(solution)/shard_map/reduce_max | solution.py:79
  152.5 4.6 %all-to-all-start.2 = ((f32[8,1,16]{2,1,0:T(1,128)}), f32[8,1,16]{2,1,0:T(1,128)S(1)}, u32[]{:S(2)}, u32[]{:S(2)}) async-start(f32[8,1,16]{2,1,0:T(1,128)} %broadcast_in_dim.42), calls=%async_computation.2 | async-start | bytes 8192 | tf_op jit(solution)/shard_map/all_to_all | solution.py:23
  157.0 7.0 %copy.41 = f32[1,8,7,128,256]{3,2,4,1,0:T(8,128)} copy(bf16[1,8,7,128,256]{4,3,2,1,0:T(8,128)(2,1)} %bitcast.124) | data formatting | bytes 11010048 | tf_op jit(solution)/shard_map/convert_element_type | solution.py:112
  164.0 9.2 %reshape.658 = f32[1,896,256,8]{1,3,2,0:T(8,128)} reshape(f32[1,7,128,8,256]{2,1,4,3,0:T(8,128)} %bitcast.136) | data formatting | bytes 14680064 | tf_op jit(solution)/shard_map/convert_element_type | solution.py:112
  173.3 9.3 %reshape.665 = f32[1,896,2048]{1,2,0:T(8,128)} reshape(f32[1,7,128,8,256]{2,1,4,3,0:T(8,128)} %bitcast.137) | data formatting | bytes 14680064 | tf_op jit(solution)/shard_map/convert_element_type | solution.py:112
  182.5 8.6 %copy.49 = f32[1,896,2048]{2,1,0:T(8,128)} copy(f32[1,896,2048]{1,2,0:T(8,128)} %reshape.665) | data formatting | bytes 14680064 | tf_op jit(solution)/shard_map/convert_element_type | solution.py:112
  191.9 19.5 %fusion.3 = (f32[896,256]{0,1:T(8,128)S(1)}, f32[896,256]{0,1:T(8,128)S(1)}, f32[896,256]{0,1:T(8,128)S(1)}, f32[896,256]{0,1:T(8,128)S(1)}, f32[896,256]{0,1:T(8,128)S(1)}, /*index=5*/f32[896,256]{0,1:T(8,128)S(1)}) fusion(f32[1,896,256,8]{1,3,2,0:T(8,128)} %reshape.658, f32[256,8]{1,0:T(8,128)S(1)} %mul.272), kind=kLoop, calls=%fused_computation.9 | loop fusion | flops 29818880 | bytes 12853248 | tf_op jit(solution)/shard_map/reduce_sum | solution.py:59
  211.4 1.9 multiply_reduce_fusion.2
  214.5 5.1 %all-to-all-start.3 = ((f32[8,1,1]{2,1,0:T(1,128)}), f32[8,1,1]{2,1,0:T(1,128)S(1)}, u32[]{:S(2)}, u32[]{:S(2)}) async-start(f32[8,1,1]{2,1,0:T(1,128)} %broadcast_in_dim.44), calls=%async_computation.3 | async-start | bytes 8192 | tf_op jit(solution)/shard_map/all_to_all | solution.py:23
  219.7 5.9 %multiply_convert_fusion = bf16[1,896,2048]{2,1,0:T(8,128)(2,1)} fusion(f32[1,896,2048]{2,1,0:T(8,128)} %copy.49, f32[2048]{0:T(1024)S(1)} %select_reduce_fusion), kind=kLoop, calls=%fused_computation.10 | loop fusion | flops 3670016 | bytes 11018240 | tf_op jit(solution)/shard_map/convert_element_type | solution.py:119
  227.4 8.7 %all-to-all-start.4 = ((f32[16,1,1]{2,1,0:T(1,128)}), f32[16,1,1]{2,1,0:T(1,128)S(1)}, u32[]{:S(2)}, u32[]{:S(2)}) async-start(f32[16,1,1]{2,1,0:T(1,128)} %broadcast_in_dim.45), calls=%async_computation.4 | async-start | bytes 16384 | tf_op jit(solution)/shard_map/all_to_all | solution.py:23
  237.4 5.8 %all-to-all-done.4 = f32[16,1,1]{2,1,0:T(1,128)S(1)} async-done(((f32[16,1,1]{2,1,0:T(1,128)}), f32[16,1,1]{2,1,0:T(1,128)S(1)}, u32[]{:S(2)}, u32[]{:S(2)}) %all-to-all-start.4) | async-done | bytes 96 | tf_op jit(solution)/shard_map/all_to_all | solution.py:23
  (30 shorter events, 18.7 us)
Async XLA Ops:
  37.0 49.9 %all-to-all-start = ((bf16[8,1,7,128,256]{4,3,2,1,0:T(8,128)(2,1)}), bf16[8,1,7,128,256]{4,3,2,1,0:T(8,128)(2,1)}, u32[]{:S(2)}, u32[]{:S(2)}) async-start(bf16[8,1,7,128,256]{4,3,2,1,0:T(8,128)(2,1)} %fusion.21), calls=%async_computation | async-start | bytes 7340032 | tf_op jit(solution)/shard_map/all_to_all | solution.py:17
  101.8 46.7 %all-to-all-start.1 = ((bf16[1,56,128,256]{3,2,0,1:T(8,128)(2,1)}), bf16[1,56,128,256]{3,2,0,1:T(8,128)(2,1)}, u32[]{:S(2)}, u32[]{:S(2)}) async-start(bf16[1,56,128,256]{3,2,0,1:T(8,128)(2,1)} %fusion.6), calls=%async_computation.1 | async-start | bytes 7340032 | tf_op jit(solution)/shard_map/all_to_all | solution.py:110
  106.3 45.4 %copy-start = (s32[1,2048]{1,0:T(1,128)S(1)}, s32[1,2048]{1,0:T(1,128)}, u32[]{:S(2)}) copy-start(s32[1,2048]{1,0:T(1,128)} %param.7) | copy-start | bytes 24580
  152.5 38.7 %all-to-all-start.2 = ((f32[8,1,16]{2,1,0:T(1,128)}), f32[8,1,16]{2,1,0:T(1,128)S(1)}, u32[]{:S(2)}, u32[]{:S(2)}) async-start(f32[8,1,16]{2,1,0:T(1,128)} %broadcast_in_dim.42), calls=%async_computation.2 | async-start | bytes 8192 | tf_op jit(solution)/shard_map/all_to_all | solution.py:23
  214.5 11.1 %all-to-all-start.3 = ((f32[8,1,1]{2,1,0:T(1,128)}), f32[8,1,1]{2,1,0:T(1,128)S(1)}, u32[]{:S(2)}, u32[]{:S(2)}) async-start(f32[8,1,1]{2,1,0:T(1,128)} %broadcast_in_dim.44), calls=%async_computation.3 | async-start | bytes 8192 | tf_op jit(solution)/shard_map/all_to_all | solution.py:23
  227.4 15.7 %all-to-all-start.4 = ((f32[16,1,1]{2,1,0:T(1,128)}), f32[16,1,1]{2,1,0:T(1,128)S(1)}, u32[]{:S(2)}, u32[]{:S(2)}) async-start(f32[16,1,1]{2,1,0:T(1,128)} %broadcast_in_dim.45), calls=%async_computation.4 | async-start | bytes 16384 | tf_op jit(solution)/shard_map/all_to_all | solution.py:23
